TPU v7x, 32 devices: a whole 2x2x4 slice. The times are simulated.
32 devices in a mesh: cluster: 4 (over x, core), leaf: 8 (over z, y).
Axes of the slice: x: 2, y: 2, z: 4, core: 2. Of those that a mesh axis runs over, the one named last changes fastest.
Arguments:
- probes: float32 [32768, 512], P(('cluster', 'leaf')), may hold values from -6 to 6
- dense_leaf: float32 [32768, 1024], P(('cluster', 'leaf')), may hold values from -0.1875 to 0.1875
- leaf_basis: float32 [32768, 128], P(('cluster', 'leaf')), may hold values from -0.1875 to 0.1875
- sibling_cores: float32 [32, 8, 128, 128], P(('cluster', 'leaf')), may hold values from -0.5 to 0.5
- transfer: float32 [32, 128, 128], P(('cluster', 'leaf')), may hold values from -0.5 to 0.5
- cluster_cores: float32 [4, 4, 128, 128], P('cluster'), may hold values from -0.1875 to 0.1875
Outputs:
- product: float32 [32768, 512], P(('cluster', 'leaf'))
All inputs are finite; a program needn't handle non-finite values.
Results may differ from a plain program's by a relative error of at most 0.00005.
Values sent between devices are 32-bit elements; how exact they have to be, the bound alone decides.
No kernel may reach another device: no remote copies, remote signals or barrier semaphores. Data moves between devices by JAX's collectives and lax.ppermute only.
A program may use at most 128 MiB of HBM per device.

v0:
```python
import jax
import jax.numpy as jnp
from jax import lax
from jax.sharding import PartitionSpec as P

HI = lax.Precision.HIGHEST


def local(probes, dense_leaf, leaf_basis, sibling_cores, transfer, cluster_cores):
    own = lax.axis_index("leaf")
    cown = lax.axis_index("cluster")
    cores = sibling_cores[0]
    trans = transfer[0]
    outer_cores = cluster_cores[0]
    rank_two = trans.shape[1]
    near = jnp.dot(dense_leaf, probes, precision=HI) + jnp.dot(dense_leaf.T, probes, precision=HI)
    coef = jnp.dot(leaf_basis.T, probes, precision=HI)
    turned = lax.all_to_all(cores, "leaf", split_axis=0, concat_axis=0, tiled=True)
    used = cores + jnp.transpose(turned, (0, 2, 1))
    piece = lax.all_gather(coef[None], "leaf", axis=0, tiled=True)
    count = piece.shape[0]
    block = used
    keep = (jnp.arange(count, dtype=jnp.int32) != own).astype(jnp.float32)
    block = block * keep[:, None, None]
    sib = jnp.einsum("jab,jbp->ap", block, piece, precision=HI)
    local_g = jnp.dot(trans.T, coef, precision=HI)
    nclu = outer_cores.shape[0]
    bkeep = (jnp.arange(nclu, dtype=jnp.int32) != cown).astype(jnp.float32)[:, None, None]
    masked = outer_cores * bkeep
    g_whole = lax.psum(local_g, "leaf")
    gathered = lax.all_gather(g_whole[None], "cluster", axis=0, tiled=True)
    front = jnp.einsum("dab,dbp->ap", masked, gathered, precision=HI)
    number = rank_two * lax.axis_size("cluster") // rank_two
    block = masked
    terms = jnp.einsum("dba,bp->dap", block, g_whole, precision=HI)
    field = front + lax.psum_scatter(
        terms.reshape(number * rank_two, g_whole.shape[1]),
        "cluster",
        scatter_dimension=0,
        tiled=True,
    )
    total = sib + jnp.dot(trans, field, precision=HI)
    return near + jnp.dot(leaf_basis, total, precision=HI)


def solution(mesh):
    return jax.shard_map(
        local,
        mesh=mesh,
        in_specs=(
            P(("cluster", "leaf"), None),
            P(("cluster", "leaf"), None),
            P(("cluster", "leaf"), None),
            P(("cluster", "leaf"), None, None, None),
            P(("cluster", "leaf"), None, None),
            P("cluster", None, None, None),
        ),
        out_specs=P(("cluster", "leaf"), None),
        check_vma=False,
    )
```

profile of v0, /device:TPU:0, one launch (start us, length us, event | category | flops | bytes accessed | tf_op | source)
XLA Modules:
  0.0 197.5 jit_solution(9313554170039844846)
XLA Ops:
  6.5 0.0 copy-start
  6.5 0.0 all-reduce.2.cloned.1.call-start
  6.5 1.6 copy-done
  8.1 2.4 %fusion.10 = f32[128,512]{1,0:T(8,128)S(1)} fusion(f32[1024,128]{1,0:T(8,128)} %param.8, f32[1024,512]{1,0:T(8,128)S(1)} %copy-done), kind=kOutput, calls=%fused_computation.18 | convolution fusion | flops 805306368 | bytes 2883584 | tf_op jit(solution)/shard_map/dot_general | solution.py:17
  10.5 0.0 copy-start.3
  10.6 0.0 copy-done.6
  10.6 1.3 convolution_bitcast_fusion.3
  11.9 0.0 all-reduce.2.cloned.1.call-update
  11.9 0.0 all-gather.7.cloned.1.call-start
  11.9 73.8 %all-reduce.2.cloned.1.call-done = f32[128,512]{0,1:T(8,128)} async-done(((f32[128,512]{0,1:T(8,128)}), f32[128,512]{0,1:T(8,128)}) %all-reduce.2.cloned.1.call-update) | async-done | bytes 262160 | tf_op jit(solution)/shard_map/psum | solution.py:30
  85.8 0.0 all-gather.7.cloned.1.call-update
  85.8 0.0 reduce-scatter.2.cloned.1.call-start
  85.8 0.0 copy-done.5
  85.8 0.1 copy.10
  86.0 0.1 bitcast_multiply_fusion
  86.1 2.9 %fusion.11 = f32[512,512]{1,0:T(8,128)} fusion(f32[512,128]{1,0:T(8,128)S(1)} %bitcast.52, f32[128,512]{0,1:T(8,128)} %all-reduce.2.cloned.1.call-done), kind=kOutput, calls=%fused_computation.19 | convolution fusion | flops 402653184 | bytes 1572864 | tf_op jit(solution)/shard_map/dba,bp->dap/dot_general | solution.py:35
  89.0 0.0 reduce-scatter.2.cloned.1.call-update
  89.0 0.0 copy-done.3
  89.1 0.0 all-gather.5.cloned.1.call-start
  89.1 0.5 all-gather.5.cloned.1.call-update
  89.6 1.0 copy.9
  90.6 4.3 %all-to-all-start = ((f32[8,128,128]{1,2,0:T(8,128)}), f32[8,128,128]{1,2,0:T(8,128)}, u32[]{:S(2)}, u32[]{:S(2)}) async-start(f32[8,128,128]{1,2,0:T(8,128)} %copy.9), calls=%async_computation | async-start | bytes 1048576 | tf_op jit(solution)/shard_map/all_to_all | solution.py:18
  95.0 9.6 %fusion.8 = f32[1024,512]{1,0:T(8,128)} fusion(f32[1024,1024]{1,0:T(8,128)} %param.7, f32[1024,512]{1,0:T(8,128)S(1)} %copy-done), kind=kOutput, calls=%fused_computation.16 | convolution fusion | flops 6442450944 | bytes 8388608 | tf_op jit(solution)/shard_map/dot_general | solution.py:16
  104.6 9.6 %fusion.9 = f32[1024,512]{1,0:T(8,128)} fusion(f32[1024,1024]{1,0:T(8,128)} %param.7, f32[1024,512]{1,0:T(8,128)S(1)} %copy-done), kind=kOutput, calls=%fused_computation.17 | convolution fusion | flops 6442450944 | bytes 8388608 | tf_op jit(solution)/shard_map/dot_general | solution.py:16
  114.2 1.6 copy.14
  115.8 15.0 %reduce-scatter.2.cloned.1.call-done = f32[128,512]{1,0:T(8,128)} async-done(((f32[512,512]{1,0:T(8,128)}), f32[128,512]{1,0:T(8,128)}) %reduce-scatter.2.cloned.1.call-update) | async-done | bytes 262160 | tf_op jit(solution)/shard_map/reduce_scatter | solution.py:36
  130.7 2.4 %fusion.1 = f32[128,512]{1,0:T(8,128)} fusion(f32[128,512]{1,0:T(8,128)} %reduce-scatter.2.cloned.1.call-done, f32[4,128,128]{1,2,0:T(8,128)S(1)} %bitcast_multiply_fusion, f32[4,128,512]{2,1,0:T(8,128)S(1)} %bitcast.51), kind=kOutput, calls=%fused_computation.6 | convolution fusion | flops 402718720 | bytes 1835008 | tf_op jit(solution)/shard_map/dab,dbp->ap/dot_general | solution.py:32
  133.1 0.0 all-to-all-done
  133.1 48.7 %all-gather.5.cloned.1.call-done = f32[1024,512]{1,0:T(8,128)} async-done(((f32[128,512]{1,0:T(8,128)}), f32[1024,512]{1,0:T(8,128)}) %all-gather.5.cloned.1.call-update) | async-done | bytes 2097168 | tf_op jit(solution)/shard_map/all_gather | solution.py:20
  181.8 3.4 %convolution_bitcast_fusion = f32[128,512]{1,0:T(8,128)S(1)} fusion(f32[8,128,512]{2,1,0:T(8,128)} %bitcast.53, f32[8,128,128]{1,2,0:T(8,128)} %all-to-all-done, f32[8]{0:T(128)S(1)} %compare_convert_fusion.1, f32[1,8,128,128]{3,2,1,0:T(8,128)} %param.9), kind=kOutput, calls=%fused_computation.1 | convolution fusion | flops 805568512 | bytes 3407904 | tf_op jit(solution)/shard_map/jab,jbp->ap/dot_general | solution.py:25
  185.2 1.3 fusion
  186.6 4.4 %bitcast_add_fusion = f32[1024,512]{1,0:T(8,128)} fusion(f32[1024,512]{1,0:T(8,128)S(1)} %copy-done.2, f32[1024,512]{1,0:T(8,128)S(1)} %copy-done.1, f32[128,512]{1,0:T(8,128)S(1)} %fusion, f32[1024,128]{1,0:T(8,128)} %param.8), kind=kOutput, calls=%fused_computation | convolution fusion | flops 806354944 | bytes 7077888 | tf_op jit(solution)/shard_map/dot_general | solution.py:43
  (11 shorter events, 0.0 us)
Async XLA Ops:
  6.5 1.6 copy-start
  6.5 4.0 %copy-start.6 = (f32[1,128,128]{2,1,0:T(8,128)S(1)}, f32[1,128,128]{2,1,0:T(8,128)}, u32[]{:S(2)}) copy-start(f32[1,128,128]{2,1,0:T(8,128)} %param.10) | copy-start | bytes 196612
  6.5 79.3 %copy-start.5 = (f32[1,4,128,128]{3,2,1,0:T(8,128)S(1)}, f32[1,4,128,128]{3,2,1,0:T(8,128)}, u32[]{:S(2)}) copy-start(f32[1,4,128,128]{3,2,1,0:T(8,128)} %param.11) | copy-start | bytes 786436
  6.5 79.2 %all-reduce.2.cloned.1.call-start = ((), (), s32[]{:S(2)}) async-start(), calls=%async_computation.2 | async-start | bytes 524288 | tf_op jit(solution)/shard_map/psum | solution.py:30
  10.5 78.5 %copy-start.3 = (f32[128,512]{1,0:T(8,128)}, f32[128,512]{1,0:T(8,128)S(1)}, u32[]{:S(2)}) copy-start(f32[128,512]{1,0:T(8,128)S(1)} %fusion.10) | copy-start | bytes 786436
  11.9 102.3 %all-gather.7.cloned.1.call-start = ((), (), s32[]{:S(2)}) async-start(), calls=%async_computation.5 | async-start | bytes 1310720 | tf_op jit(solution)/shard_map/all_gather | solution.py:31
  85.8 3.9 %copy-start.4 = (f32[1,8,128,128]{3,2,1,0:T(8,128)S(1)}, f32[1,8,128,128]{3,2,1,0:T(8,128)}, u32[]{:S(2)}) copy-start(f32[1,8,128,128]{3,2,1,0:T(8,128)} %param.9) | copy-start | bytes 1572868
  85.8 44.9 %reduce-scatter.2.cloned.1.call-start = ((), (), s32[]{:S(2)}) async-start(), calls=%async_computation.3 | async-start | bytes 1310720 | tf_op jit(solution)/shard_map/reduce_scatter | solution.py:36
  89.1 92.8 %all-gather.5.cloned.1.call-start = ((), (), s32[]{:S(2)}) async-start(), calls=%async_computation.4 | async-start | bytes 2359296 | tf_op jit(solution)/shard_map/all_gather | solution.py:20
  90.6 42.5 %all-to-all-start = ((f32[8,128,128]{1,2,0:T(8,128)}), f32[8,128,128]{1,2,0:T(8,128)}, u32[]{:S(2)}, u32[]{:S(2)}) async-start(f32[8,128,128]{1,2,0:T(8,128)} %copy.9), calls=%async_computation | async-start | bytes 1048576 | tf_op jit(solution)/shard_map/all_to_all | solution.py:18
  181.8 4.7 %copy-start.1 = (f32[1024,512]{1,0:T(8,128)S(1)}, f32[1024,512]{1,0:T(8,128)}, u32[]{:S(2)}) copy-start(f32[1024,512]{1,0:T(8,128)} %fusion.9) | copy-start | bytes 6291460
  181.8 4.7 %copy-start.2 = (f32[1024,512]{1,0:T(8,128)S(1)}, f32[1024,512]{1,0:T(8,128)}, u32[]{:S(2)}) copy-start(f32[1024,512]{1,0:T(8,128)} %fusion.8) | copy-start | bytes 6291460
Sparse Core Ops, SparseCore 0:
  12.0 73.7 all-reduce.1
  87.3 16.0 all-gather.6
  105.9 24.7 reduce-scatter.1
  132.7 49.0 all-gather.4
where the time goes:
time: 198 us; the launch traced here: 197 us
  waiting for transfers between devices  138 us (70%)
  matrix products  37.3 us (19%)
  between operations  13.3 us (7%)
  starting transfers between devices  4.44 us (2%)
  local copies, waits for them, and re-layouts  4.31 us (2%)
    psum x1, waiting for transfers between devices, local(): g_whole = lax.psum(local_g, 'leaf')  73.8 us
    all_gather x1, waiting for transfers between devices, local(): piece = lax.all_gather(coef[None], 'leaf', axis=0, tiled=True)  48.7 us
    reduce_scatter x1, waiting for transfers between devices, local(): lax.psum_scatter(terms.reshape(number * rank_two, g_whole.shape[1]), 'clu...  15 us
    dot_general x1, matrix products, local(): jnp.dot(dense_leaf.T, probes, precision=HI)  9.6 us
    dot_general x1, matrix products, local(): jnp.dot(dense_leaf, probes, precision=HI)  9.59 us
    dot_general x1, matrix products, local(): return near + jnp.dot(leaf_basis, total, precision=HI)  4.38 us
    all_to_all x1, starting transfers between devices, local(): lax.all_to_all(cores, 'leaf', split_axis=0, concat_axis=0, tiled=True)  4.32 us
  transfers between devices with their start and end apart: 5, of which 3 were waited for; matrix products, arithmetic and copies ran while one was open for 14% of the time, Pallas kernels for 0%

commit v1 on v0

--- a/solution.py
+++ b/solution.py
@@ -4,6 +4,12 @@
 from jax.sharding import PartitionSpec as P
 
 HI = lax.Precision.HIGHEST
+
+
+def summed_here(array, name):
+    parts = lax.all_gather(array, name, axis=0, tiled=False)
+    total = parts.sum(axis=0)
+    return total
 
 
 def local(probes, dense_leaf, leaf_basis, sibling_cores, transfer, cluster_cores):
@@ -27,7 +33,7 @@
     nclu = outer_cores.shape[0]
     bkeep = (jnp.arange(nclu, dtype=jnp.int32) != cown).astype(jnp.float32)[:, None, None]
     masked = outer_cores * bkeep
-    g_whole = lax.psum(local_g, "leaf")
+    g_whole = summed_here(local_g, "leaf")
     gathered = lax.all_gather(g_whole[None], "cluster", axis=0, tiled=True)
     front = jnp.einsum("dab,dbp->ap", masked, gathered, precision=HI)
     number = rank_two * lax.axis_size("cluster") // rank_two

time: 198 us -> 181 us (0.914)
  waiting for transfers between devices: 138 us -> 119 us
  local copies, waits for them, and re-layouts: 4.31 us -> 6.37 us
    psum x1 -> x0, waiting for transfers between devices: 73.8 us -> none  [local(): g_whole = lax.psum(local_g, 'leaf')]
    all_gather x0 -> x1, waiting for transfers between devices: none -> 52.4 us  [summed_here(): parts = lax.all_gather(array, name, axis=0, tiled=False)]
    all_gather x1, waiting for transfers between devices: 48.7 us -> 24.6 us  [local(): piece = lax.all_gather(coef[None], 'leaf', axis=0, tiled=True)]
    all_gather x1, waiting for transfers between devices: 0.01 us -> 13.3 us  [local(): gathered = lax.all_gather(g_whole[None], 'cluster', axis=0, tiled=True)]
    reduce_scatter x1, waiting for transfers between devices: 15 us -> 25.6 us  [local(): lax.psum_scatter(terms.reshape(number * rank_two, g_whole.shape[1]), 'clu...]
    all_to_all x1, waiting for transfers between devices: 0.01 us -> 2.77 us  [local(): lax.all_to_all(cores, 'leaf', split_axis=0, concat_axis=0, tiled=True)]
    unnamed x15 -> x18, local copies, waits for them, and re-layouts: 1.73 us -> 3.8 us
  transfers between devices with their start and end apart: 5 -> 5, of which waited for: 3 -> 5; matrix products, arithmetic and copies ran while one was open for 14% -> 17% of each run, Pallas kernels for 0% -> 0%
where the time goes in v1:
time: 181 us; the launch traced here: 180 us
  waiting for transfers between devices  119 us (66%)
  matrix products  36.2 us (20%)
  between operations  13.3 us (7%)
  local copies, waits for them, and re-layouts  6.37 us (4%)
  starting transfers between devices  3.61 us (2%)
    all_gather x1, waiting for transfers between devices, summed_here(): parts = lax.all_gather(array, name, axis=0, tiled=False)  52.4 us
    reduce_scatter x1, waiting for transfers between devices, local(): lax.psum_scatter(terms.reshape(number * rank_two, g_whole.shape[1]), 'clu...  25.6 us
    all_gather x1, waiting for transfers between devices, local(): piece = lax.all_gather(coef[None], 'leaf', axis=0, tiled=True)  24.6 us
    all_gather x1, waiting for transfers between devices, local(): gathered = lax.all_gather(g_whole[None], 'cluster', axis=0, tiled=True)  13.3 us
    dot_general x1, matrix products, local(): jnp.dot(dense_leaf, probes, precision=HI)  9.74 us
    dot_general x1, matrix products, local(): jnp.dot(dense_leaf.T, probes, precision=HI)  8.13 us
    dot_general x1, matrix products, local(): return near + jnp.dot(leaf_basis, total, precision=HI)  4.89 us
    unnamed x18, local copies, waits for them, and re-layouts  3.8 us
  transfers between devices with their start and end apart: 5, of which 5 were waited for; matrix products, arithmetic and copies ran while one was open for 17% of the time, Pallas kernels for 0%

profile of v1, /device:TPU:0, one launch (start us, length us, event | category | flops | bytes accessed | tf_op | source)
XLA Modules:
  0.0 180.3 jit_solution(5109149889135204773)
XLA Ops:
  6.5 1.6 copy-done
  8.1 2.4 %fusion.10 = f32[128,512]{1,0:T(8,128)S(1)} fusion(f32[1024,128]{1,0:T(8,128)} %param.8, f32[1024,512]{1,0:T(8,128)S(1)} %copy-done), kind=kOutput, calls=%fused_computation.19 | convolution fusion | flops 805306368 | bytes 2883584 | tf_op jit(solution)/shard_map/dot_general | solution.py:23
  10.6 1.3 convolution_bitcast_fusion.3
  11.9 0.0 all-gather.9.cloned.1.call-update
  11.9 0.0 all-gather.7.cloned.1.call-start
  11.9 0.7 all-gather.7.cloned.1.call-update
  12.6 0.0 all-gather.11.cloned.1.call-start
  12.7 52.4 %all-gather.9.cloned.1.call-done = f32[1024,512]{0,1:T(8,128)} async-done(((f32[128,512]{0,1:T(8,128)}), f32[1024,512]{0,1:T(8,128)}) %all-gather.9.cloned.1.call-update) | async-done | bytes 2097168 | tf_op jit(solution)/shard_map/all_gather | solution.py:10
  65.1 2.1 %copy.21 = f32[64,8,8,128]{3,2,1,0:T(8,128)S(1)} copy(f32[64,8,8,128]{3,1,2,0:T(8,128)} %bitcast.59) | data formatting | bytes 4194304
  67.2 0.0 copy-start.6
  67.2 1.2 bitcast_reduce_fusion
  68.4 0.0 all-gather.11.cloned.1.call-update
  68.4 0.0 reduce-scatter.2.cloned.1.call-start
  68.5 0.1 copy.13
  68.6 0.1 bitcast_multiply_fusion
  68.7 2.9 %fusion.11 = f32[512,512]{1,0:T(8,128)} fusion(f32[512,128]{1,0:T(8,128)S(1)} %bitcast.57, f32[128,512]{0,1:T(8,128)} %bitcast_reduce_fusion), kind=kOutput, calls=%fused_computation.20 | convolution fusion | flops 402653184 | bytes 1572864 | tf_op jit(solution)/shard_map/dba,bp->dap/dot_general | solution.py:41
  71.7 0.0 reduce-scatter.2.cloned.1.call-update
  71.7 0.0 copy-done.5
  71.7 1.0 copy.12
  72.7 3.5 %all-to-all-start = ((f32[8,128,128]{1,2,0:T(8,128)}), f32[8,128,128]{1,2,0:T(8,128)S(1)}, u32[]{:S(2)}, u32[]{:S(2)}) async-start(f32[8,128,128]{1,2,0:T(8,128)} %copy.12), calls=%async_computation | async-start | bytes 1048576 | tf_op jit(solution)/shard_map/all_to_all | solution.py:24
  76.2 0.0 copy-start.1
  76.3 9.7 %fusion.8 = f32[1024,512]{1,0:T(8,128)} fusion(f32[1024,1024]{1,0:T(8,128)} %param.7, f32[1024,512]{1,0:T(8,128)S(1)} %copy-done), kind=kOutput, calls=%fused_computation.17 | convolution fusion | flops 6442450944 | bytes 8388608 | tf_op jit(solution)/shard_map/dot_general | solution.py:22
  86.0 8.1 %fusion.9 = f32[1024,512]{1,0:T(8,128)} fusion(f32[1024,1024]{1,0:T(8,128)S(1)} %copy-done.1, f32[1024,512]{1,0:T(8,128)S(1)} %copy-done), kind=kOutput, calls=%fused_computation.18 | convolution fusion | flops 6442450944 | bytes 8388608 | tf_op jit(solution)/shard_map/dot_general | solution.py:22
  94.1 2.8 %all-to-all-done = f32[8,128,128]{1,2,0:T(8,128)S(1)} async-done(((f32[8,128,128]{1,2,0:T(8,128)}), f32[8,128,128]{1,2,0:T(8,128)S(1)}, u32[]{:S(2)}, u32[]{:S(2)}) %all-to-all-start) | async-done | bytes 524320 | tf_op jit(solution)/shard_map/all_to_all | solution.py:24
  96.9 24.6 %all-gather.7.cloned.1.call-done = f32[1024,512]{1,0:T(8,128)} async-done(((f32[128,512]{1,0:T(8,128)}), f32[1024,512]{1,0:T(8,128)}) %all-gather.7.cloned.1.call-update) | async-done | bytes 2097168 | tf_op jit(solution)/shard_map/all_gather | solution.py:26
  121.4 3.6 %convolution_bitcast_fusion = f32[128,512]{1,0:T(8,128)} fusion(f32[8,128,512]{2,1,0:T(8,128)} %bitcast.58, f32[8,128,128]{1,2,0:T(8,128)S(1)} %all-to-all-done, f32[8]{0:T(128)S(1)} %compare_convert_fusion.1, f32[1,8,128,128]{3,2,1,0:T(8,128)S(1)} %copy-done.5), kind=kOutput, calls=%fused_computation.2 | convolution fusion | flops 805568512 | bytes 3407904 | tf_op jit(solution)/shard_map/jab,jbp->ap/dot_general | solution.py:31
  125.1 13.3 %all-gather.11.cloned.1.call-done = f32[512,512]{0,1:T(8,128)} async-done(((f32[128,512]{0,1:T(8,128)}), f32[512,512]{0,1:T(8,128)}) %all-gather.11.cloned.1.call-update) | async-done | bytes 1048592 | tf_op jit(solution)/shard_map/all_gather | solution.py:37
  138.4 1.6 copy.14
  139.9 25.6 %reduce-scatter.2.cloned.1.call-done = f32[128,512]{1,0:T(8,128)} async-done(((f32[512,512]{1,0:T(8,128)}), f32[128,512]{1,0:T(8,128)}) %reduce-scatter.2.cloned.1.call-update) | async-done | bytes 262160 | tf_op jit(solution)/shard_map/reduce_scatter | solution.py:42
  165.6 1.9 %fusion.1 = f32[128,512]{1,0:T(8,128)S(1)} fusion(f32[128,512]{1,0:T(8,128)} %reduce-scatter.2.cloned.1.call-done, f32[4,128,128]{1,2,0:T(8,128)S(1)} %bitcast_multiply_fusion, f32[4,128,512]{2,1,0:T(8,128)S(1)} %bitcast.56), kind=kOutput, calls=%fused_computation.7 | convolution fusion | flops 402718720 | bytes 1835008 | tf_op jit(solution)/shard_map/dab,dbp->ap/dot_general | solution.py:38
  167.5 1.3 fusion
  168.8 4.9 %bitcast_add_fusion = f32[1024,512]{1,0:T(8,128)} fusion(f32[1024,512]{1,0:T(8,128)} %fusion.8, f32[1024,512]{1,0:T(8,128)S(1)} %copy-done.2, f32[128,512]{1,0:T(8,128)S(1)} %fusion, f32[1024,128]{1,0:T(8,128)S(1)} %copy-done.4), kind=kOutput, calls=%fused_computation.1 | convolution fusion | flops 806354944 | bytes 7077888 | tf_op jit(solution)/shard_map/dot_general | solution.py:49
  (15 shorter events, 0.0 us)
Async XLA Ops:
  6.5 1.6 copy-start
  6.5 4.0 %copy-start.7 = (f32[1,128,128]{2,1,0:T(8,128)S(1)}, f32[1,128,128]{2,1,0:T(8,128)}, u32[]{:S(2)}) copy-start(f32[1,128,128]{2,1,0:T(8,128)} %param.10) | copy-start | bytes 196612
  6.5 58.6 %all-gather.9.cloned.1.call-start = ((), (), s32[]{:S(2)}) async-start(), calls=%async_computation.4 | async-start | bytes 2359296 | tf_op jit(solution)/shard_map/all_gather | solution.py:10
  10.5 1.4 copy-start.3
  11.9 109.6 %all-gather.7.cloned.1.call-start = ((), (), s32[]{:S(2)}) async-start(), calls=%async_computation.3 | async-start | bytes 2359296 | tf_op jit(solution)/shard_map/all_gather | solution.py:26
  12.6 125.7 %all-gather.11.cloned.1.call-start = ((), (), s32[]{:S(2)}) async-start(), calls=%async_computation.5 | async-start | bytes 1310720 | tf_op jit(solution)/shard_map/all_gather | solution.py:37
  67.2 1.3 copy-start.6
  68.4 3.3 %copy-start.5 = (f32[1,8,128,128]{3,2,1,0:T(8,128)S(1)}, f32[1,8,128,128]{3,2,1,0:T(8,128)}, u32[]{:S(2)}) copy-start(f32[1,8,128,128]{3,2,1,0:T(8,128)} %param.9) | copy-start | bytes 1572868
  68.4 97.2 %reduce-scatter.2.cloned.1.call-start = ((), (), s32[]{:S(2)}) async-start(), calls=%async_computation.2 | async-start | bytes 1310720 | tf_op jit(solution)/shard_map/reduce_scatter | solution.py:42
  72.7 24.2 %all-to-all-start = ((f32[8,128,128]{1,2,0:T(8,128)}), f32[8,128,128]{1,2,0:T(8,128)S(1)}, u32[]{:S(2)}, u32[]{:S(2)}) async-start(f32[8,128,128]{1,2,0:T(8,128)} %copy.12), calls=%async_computation | async-start | bytes 1048576 | tf_op jit(solution)/shard_map/all_to_all | solution.py:24
  76.2 9.8 %copy-start.1 = (f32[1024,1024]{1,0:T(8,128)S(1)}, f32[1024,1024]{1,0:T(8,128)}, u32[]{:S(2)}) copy-start(f32[1024,1024]{1,0:T(8,128)} %param.7) | copy-start | bytes 12582916
  165.6 3.2 %copy-start.2 = (f32[1024,512]{1,0:T(8,128)S(1)}, f32[1024,512]{1,0:T(8,128)}, u32[]{:S(2)}) copy-start(f32[1024,512]{1,0:T(8,128)} %fusion.9) | copy-start | bytes 6291460
  165.6 3.2 %copy-start.4 = (f32[1024,128]{1,0:T(8,128)S(1)}, f32[1024,128]{1,0:T(8,128)}, u32[]{:S(2)}) copy-start(f32[1024,128]{1,0:T(8,128)} %param.8) | copy-start | bytes 1572868
Sparse Core Ops, SparseCore 0:
  12.0 53.0 all-gather.8
  67.2 54.1 all-gather.6
  123.0 15.3 all-gather.10
  140.8 24.7 reduce-scatter.1
